TPU v7x, 8 devices: a whole 2x2x1 slice. The times are simulated.
8 devices in a mesh: tp: 2 (over z, y), dp: 4 (over x, core).
Axes of the slice: x: 2, y: 2, z: 1, core: 2. Of those that a mesh axis runs over, the one named last changes fastest.
Arguments:
- a_mat: bfloat16 [5120, 32768], P(('dp', 'tp'))
- b_mat: bfloat16 [32768, 13824], P(('dp', 'tp'))
Outputs:
- output: bfloat16 [5120, 13824], P(('dp', 'tp'))
All inputs are finite; a program needn't handle non-finite values.
Results may differ from a plain program's by a relative error of at most 0.001.
Values are sent between devices in bfloat16 or wider.
A program may use at most 1 GiB of HBM per device.

v0:
```python
import jax
import jax.numpy as jnp
from jax import lax
from jax.sharding import PartitionSpec as P


def solution(mesh):
    spec_rows = P(("dp", "tp"), None)

    def local_block(a_rows, b_rows):
        a_cols = lax.all_to_all(a_rows, "dp", 1, 0, tiled=True)
        b_slab = lax.all_gather(b_rows, "tp", axis=0, tiled=True)
        part_prod = jnp.dot(a_cols, b_slab, preferred_element_type=jnp.float32)
        summed = lax.psum_scatter(part_prod, "dp", scatter_dimension=0, tiled=True)
        return summed.astype(jnp.bfloat16)

    return jax.shard_map(local_block, mesh=mesh, in_specs=(spec_rows, spec_rows), out_specs=spec_rows, check_vma=False)
```

profile of v0, /device:TPU:0, one launch (start us, length us, event | category | flops | bytes accessed | tf_op | source)
XLA Modules:
  0.0 4114.1 jit_solution(4896686985840558027)
XLA Ops:
  6.5 0.0 all-gather.2.cloned.1.call-start
  6.5 0.7 all-gather.2.cloned.1.call-update
  7.3 0.0 reduce-scatter.2.cloned.1.call-start
  7.3 49.7 %copy.3 = bf16[640,32768]{0,1:T(8,128)(2,1)} copy(bf16[640,32768]{1,0:T(8,128)(2,1)} %param.2) | data formatting | bytes 83886080 | tf_op args[0]
  57.0 475.1 %all_to_all.19 = bf16[640,4,8192]{0,2,1:T(8,128)(2,1)} all-to-all(bf16[640,4,8192]{0,2,1:T(8,128)(2,1)} %bitcast.6), channel_id=1, replica_groups=mesh['tp'=2,'dp'=4] {'dp'}, dimensions={1} | all-to-all | bytes 83886080 | tf_op jit(solution)/shard_map/all_to_all | solution.py:11
  532.2 51.6 %copy.4 = bf16[4,640,8192]{2,1,0:T(8,128)(2,1)} copy(bf16[4,640,8192]{1,2,0:T(8,128)(2,1)} %bitcast.5) | data formatting | bytes 83886080 | tf_op jit(solution)/shard_map/all_to_all | solution.py:11
  583.7 1984.9 %all-gather.2.cloned.1.call-done = bf16[8192,13824]{1,0:T(8,128)(2,1)} async-done(((bf16[4096,13824]{1,0:T(8,128)(2,1)}), bf16[8192,13824]{1,0:T(8,128)(2,1)}) %all-gather.2.cloned.1.call-update) | async-done | bytes 226492432 | tf_op jit(solution)/shard_map/all_gather | solution.py:12
  2568.7 605.7 %fusion = f32[2560,13824]{1,0:T(8,128)} fusion(bf16[2560,8192]{1,0:T(8,128)(2,1)} %bitcast.7, bf16[8192,13824]{1,0:T(8,128)(2,1)} %all-gather.2.cloned.1.call-done), kind=kOutput, calls=%fused_computation | convolution fusion | flops 579820584960 | bytes 409993216 | tf_op jit(solution)/shard_map/dot_general | solution.py:13
  3174.4 0.0 reduce-scatter.2.cloned.1.call-update
  3174.4 913.4 %reduce-scatter.2.cloned.1.call-done = f32[640,13824]{1,0:T(8,128)} async-done(((f32[2560,13824]{1,0:T(8,128)}), f32[640,13824]{1,0:T(8,128)}) %reduce-scatter.2.cloned.1.call-update) | async-done | bytes 35389456 | tf_op jit(solution)/shard_map/reduce_scatter | solution.py:14
  4087.9 19.4 convert_element_type.3
Async XLA Ops:
  6.5 2562.2 %all-gather.2.cloned.1.call-start = ((), (), s32[]{:S(2)}) async-start(), calls=%async_computation.2 | async-start | bytes 339738624 | tf_op jit(solution)/shard_map/all_gather | solution.py:12
  7.3 4080.6 %reduce-scatter.2.cloned.1.call-start = ((), (), s32[]{:S(2)}) async-start(), calls=%async_computation.3 | async-start | bytes 176947200 | tf_op jit(solution)/shard_map/reduce_scatter | solution.py:14
Sparse Core Ops, SparseCore 0:
  8.8 2559.7 all-gather.1
  3174.6 913.2 reduce-scatter.1
where the time goes:
time: 4120 us; the launch traced here: 4110 us
  waiting for transfers between devices  2900 us (70%)
  matrix products  606 us (15%)
  blocking collectives  475 us (12%)
  local copies, waits for them, and re-layouts  101 us (2%)
    all_gather x1, waiting for transfers between devices, local_block(): b_slab = lax.all_gather(b_rows, 'tp', axis=0, tiled=True)  1980 us
    reduce_scatter x1, waiting for transfers between devices, local_block(): summed = lax.psum_scatter(part_prod, 'dp', scatter_dimension=0, tiled=True)  913 us
    dot_general x1, matrix products, local_block(): part_prod = jnp.dot(a_cols, b_slab, preferred_element_type=jnp.float32)  606 us
    all_to_all x1, blocking collectives, local_block(): a_cols = lax.all_to_all(a_rows, 'dp', 1, 0, tiled=True)  475 us
  transfers between devices with their start and end apart: 2, of which 2 were waited for; matrix products, arithmetic and copies ran while one was open for 2% of the time, Pallas kernels for 0%

commit v1 on v0

v1 whole, which is shorter than its diff:
```python
import functools

import jax
import jax.numpy as jnp
from jax import lax
from jax.experimental import pallas as pl
from jax.experimental.pallas import tpu as pltpu
from jax.sharding import PartitionSpec as P

MESH = pl.DeviceIdType.MESH
HALF = 9
TILES = 2 * HALF
KSTEPS = 4
BCHUNKS = 4
WIDE = 256
OWN, FIRST, DIAG, SECOND = 0, 1, 2, 3


def _kernel(
    a_ref, b_ref, c_ref, a_got, b_got, part, first, fwd, last, summed,
    a_v, b_v, acc, add_v, out_v,
    a_send, a_recv, b_send, b_recv, p_send, p_recv, load_sem, b_sem, acc_sem, add_sem,
):
    rows = a_ref.shape[0]
    depth, cols = b_ref.shape
    tn = cols // TILES
    kc = depth // KSTEPS
    wide = min(WIDE, tn)

    dp, y = lax.axis_index("dp"), lax.axis_index("tp")
    x, core = dp // 2, dp % 2

    def device(dx, dc, dy):
        return {"dp": ((x + dx) % 2) * 2 + (core + dc) % 2, "tp": (y + dy) % 2}

    def a_cols(dx, dc, dy):
        block = ((x + dx) % 2) * 4 + ((core + dc) % 2) * 2 + (y + dy) % 2
        return pl.ds(pl.multiple_of(block * depth, depth), depth)

    barrier = pltpu.get_barrier_semaphore()
    for d in ((1, 0, 0), (0, 0, 1), (1, 0, 1), (0, 1, 0)):
        pl.semaphore_signal(barrier, inc=1, device_id=device(*d), device_id_type=MESH)
    pl.semaphore_wait(barrier, 4)

    bc = depth // BCHUNKS
    b_copies = [
        pltpu.make_async_remote_copy(
            src_ref=b_ref.at[pl.ds(j * bc, bc)],
            dst_ref=b_got.at[pl.ds(j * bc, bc)],
            send_sem=b_send.at[j],
            recv_sem=b_recv.at[j],
            device_id=device(0, 1, 0),
            device_id_type=MESH,
        )
        for j in range(BCHUNKS)
    ]
    a_copies = [
        [
            pltpu.make_async_remote_copy(
                src_ref=a_ref.at[:, a_cols(dx, dc, dy)],
                dst_ref=a_got.at[g, :, pl.ds(dc * depth, depth)],
                send_sem=a_send.at[g, dc],
                recv_sem=a_recv.at[g, dc],
                device_id=device(dx, 0, dy),
                device_id_type=MESH,
            )
            for dc in range(2)
        ]
        for g, (dx, dy) in enumerate(((1, 0), (0, 1), (1, 1)))
    ]
    for copy in b_copies:
        copy.start()
    for dc in range(2):
        a_copies[0][dc].start()
        a_copies[1][dc].start()
    for dc in range(2):
        a_copies[2][dc].start()

    own_loads = [
        pltpu.make_async_copy(
            a_ref.at[:, a_cols(0, dc, 0)], a_v.at[2, :, pl.ds(dc * depth, depth)], load_sem.at[dc]
        )
        for dc in range(2)
    ]
    for load in own_loads:
        load.start()
    for load in own_loads:
        load.wait()
    for copy in b_copies:
        copy.wait_recv()

    def place(i):
        return i % 2, i // 2 + HALF * (i % 2)

    def hop(par, dst, src, t, kind):
        return pltpu.make_async_remote_copy(
            src_ref=src,
            dst_ref=dst.at[t],
            send_sem=p_send.at[kind, t],
            recv_sem=p_recv.at[kind, t],
            device_id={"dp": ((x + 1 - par) % 2) * 2 + core, "tp": (y + par) % 2},
            device_id_type=MESH,
        )

    def b_loads(s):
        _, t = place(s // KSTEPS)
        k, slot = s % KSTEPS, s % 2
        at = (
            pl.ds(pl.multiple_of(k * kc, kc), kc),
            pl.ds(pl.multiple_of(t * tn, tn), tn),
        )
        return [
            pltpu.make_async_copy(ref.at[at], b_v.at[slot, h], b_sem.at[slot, h])
            for h, ref in enumerate((b_ref, b_got))
        ]

    def phase(which, a_slot, dst):
        def acc_out(i):
            _, t = place(i)
            return pltpu.make_async_copy(acc.at[i % 2], part.at[which, t], acc_sem.at[i % 2])

        def finish(i):
            acc_out(i).wait()
            if dst is not None:
                par, t = place(i)
                hop(par, dst, part.at[which, t], t, which - FIRST).start()

        for load in b_loads(0):
            load.start()

        def step(s, carry):
            i, k = s // KSTEPS, s % KSTEPS
            slot, into = s % 2, i % 2

            @pl.when(s + 1 < TILES * KSTEPS)
            def _():
                for load in b_loads(s + 1):
                    load.start()

            for load in b_loads(s):
                load.wait()
            a_at = a_slot(i % 2)
            near = pl.ds(pl.multiple_of(k * kc, kc), kc)
            far = pl.ds(pl.multiple_of(depth + k * kc, kc), kc)

            def piece(w, inner):
                at = pl.ds(pl.multiple_of(w * wide, wide), wide)
                dots = jnp.dot(
                    a_v[a_at, :, near], b_v[slot, 0, :, at], preferred_element_type=jnp.float32
                ) + jnp.dot(
                    a_v[a_at, :, far], b_v[slot, 1, :, at], preferred_element_type=jnp.float32
                )
                held = acc[into, :, at]
                acc[into, :, at] = jnp.where(k == 0, dots, held + dots)
                return inner

            lax.fori_loop(0, tn // wide, piece, 0)

            @pl.when(k == KSTEPS - 1)
            def _():
                acc_out(i).start()

                @pl.when(i > 0)
                def _():
                    finish(i - 1)

            return carry

        lax.fori_loop(0, TILES * KSTEPS, step, 0)
        finish(TILES - 1)

    def fetch(g, slot):
        for copy in a_copies[g]:
            copy.wait_recv()
        return pltpu.make_async_copy(a_got.at[g], a_v.at[slot], load_sem.at[slot])

    phase(OWN, lambda par: 2, None)
    loads = [fetch(0, 0), fetch(1, 1)]
    for load in loads:
        load.start()
    for load in loads:
        load.wait()
    phase(FIRST, lambda par: par, first)
    load = fetch(2, 2)
    load.start()
    load.wait()
    phase(DIAG, lambda par: 2, fwd)
    phase(SECOND, lambda par: 1 - par, None)

    def forward(i, carry):
        par, t = place(i)
        mine = pltpu.make_async_copy(part.at[SECOND, t], add_v.at[0], add_sem.at[0])
        mine.start()
        hop(par, fwd, part.at[DIAG, t], t, DIAG - FIRST).wait_recv()
        theirs = pltpu.make_async_copy(fwd.at[t], add_v.at[1], add_sem.at[1])
        theirs.start()
        mine.wait()
        theirs.wait()
        add_v[2] = add_v[0] + add_v[1]
        out = pltpu.make_async_copy(add_v.at[2], summed.at[t], add_sem.at[2])
        out.start()
        out.wait()
        hop(1 - par, last, summed.at[t], t, 2).start()
        return carry

    lax.fori_loop(0, TILES, forward, 0)

    def final(i, carry):
        par, t = place(i)
        own = pltpu.make_async_copy(part.at[OWN, t], add_v.at[0], add_sem.at[0])
        own.start()
        hop(par, first, part.at[FIRST, t], t, 0).wait_recv()
        near = pltpu.make_async_copy(first.at[t], add_v.at[1], add_sem.at[1])
        near.start()
        own.wait()
        near.wait()
        hop(1 - par, last, summed.at[t], t, 2).wait_recv()
        far = pltpu.make_async_copy(last.at[t], add_v.at[2], add_sem.at[2])
        far.start()
        far.wait()
        out_v[...] = (add_v[0] + add_v[1] + add_v[2]).astype(out_v.dtype)
        out = pltpu.make_async_copy(
            out_v, c_ref.at[:, pl.ds(pl.multiple_of(t * tn, tn), tn)], add_sem.at[3]
        )
        out.start()
        out.wait()
        return carry

    lax.fori_loop(0, TILES, final, 0)

    for copy in b_copies:
        copy.wait_send()
    for pair in a_copies:
        for copy in pair:
            copy.wait_send()

    def drain(i, carry):
        par, t = place(i)
        hop(par, first, part.at[FIRST, t], t, 0).wait_send()
        hop(par, fwd, part.at[DIAG, t], t, 1).wait_send()
        hop(1 - par, last, summed.at[t], t, 2).wait_send()
        return carry

    lax.fori_loop(0, TILES, drain, 0)


def solution(mesh):
    spec_rows = P(("dp", "tp"), None)

    def local_block(a_rows, b_rows):
        rows, inner = a_rows.shape
        depth, cols = b_rows.shape
        tn = cols // TILES
        f32, bf16 = jnp.float32, a_rows.dtype
        hbm = pl.BlockSpec(memory_space=pl.ANY)
        tiles = jax.ShapeDtypeStruct((TILES, rows, tn), f32)
        outs = pl.pallas_call(
            _kernel,
            out_shape=[
                jax.ShapeDtypeStruct((rows, cols), bf16),
                jax.ShapeDtypeStruct((3, rows, 2 * depth), bf16),
                jax.ShapeDtypeStruct((depth, cols), bf16),
                jax.ShapeDtypeStruct((4, TILES, rows, tn), f32),
                tiles,
                tiles,
                tiles,
                tiles,
            ],
            in_specs=[hbm] * 2,
            out_specs=[hbm] * 8,
            scratch_shapes=[
                pltpu.VMEM((3, rows, 2 * depth), bf16),
                pltpu.VMEM((2, 2, depth // KSTEPS, tn), bf16),
                pltpu.VMEM((2, rows, tn), f32),
                pltpu.VMEM((3, rows, tn), f32),
                pltpu.VMEM((rows, tn), bf16),
                pltpu.SemaphoreType.DMA((3, 2)),
                pltpu.SemaphoreType.DMA((3, 2)),
                pltpu.SemaphoreType.DMA((BCHUNKS,)),
                pltpu.SemaphoreType.DMA((BCHUNKS,)),
                pltpu.SemaphoreType.DMA((3, TILES)),
                pltpu.SemaphoreType.DMA((3, TILES)),
                pltpu.SemaphoreType.DMA((3,)),
                pltpu.SemaphoreType.DMA((2, 2)),
                pltpu.SemaphoreType.DMA((2,)),
                pltpu.SemaphoreType.DMA((4,)),
            ],
            compiler_params=pltpu.CompilerParams(
                collective_id=0, has_side_effects=True, vmem_limit_bytes=60 * 2**20
            ),
            cost_estimate=pl.CostEstimate(
                flops=2 * rows * inner * cols, bytes_accessed=2**30, transcendentals=0
            ),
        )(a_rows, b_rows)
        return outs[0]

    return jax.shard_map(local_block, mesh=mesh, in_specs=(spec_rows, spec_rows), out_specs=spec_rows, check_vma=False)
```

time: 4120 us -> 1620 us (0.39)
  waiting for transfers between devices: 2900 us -> 0 us
  Pallas kernels: 0 us -> 1600 us
  matrix products: 606 us -> 0 us
  blocking collectives: 475 us -> 0 us
  local copies, waits for them, and re-layouts: 101 us -> 15.7 us
    all_gather x1 -> x0, waiting for transfers between devices: 1980 us -> none  [local_block(): b_slab = lax.all_gather(b_rows, 'tp', axis=0, tiled=True)]
    pallas_call x0 -> x1, Pallas kernels: none -> 1600 us  [local_block(): pl.pallas_call(_kernel, out_shape=[jax.ShapeDtypeStruct((rows, cols), bf1...]
    reduce_scatter x1 -> x0, waiting for transfers between devices: 913 us -> none  [local_block(): summed = lax.psum_scatter(part_prod, 'dp', scatter_dimension=0, tiled=True)]
    dot_general x1 -> x0, matrix products: 606 us -> none  [local_block(): part_prod = jnp.dot(a_cols, b_slab, preferred_element_type=jnp.float32)]
    all_to_all x1 -> x0, blocking collectives: 475 us -> none  [local_block(): a_cols = lax.all_to_all(a_rows, 'dp', 1, 0, tiled=True)]
    all_to_all x1 -> x0, local copies, waits for them, and re-layouts: 51.6 us -> none  [local_block(): a_cols = lax.all_to_all(a_rows, 'dp', 1, 0, tiled=True)]
  transfers between devices with their start and end apart: 2 -> 0, of which waited for: 2 -> 0; matrix products, arithmetic and copies ran while one was open for 2% -> 0% of each run, Pallas kernels for 0% -> 0%
where the time goes in v1:
time: 1620 us
  Pallas kernels  1600 us (99%)
    pallas_call x1, Pallas kernels, local_block(): pl.pallas_call(_kernel, out_shape=[jax.ShapeDtypeStruct((rows, cols), bf1...  1600 us

profile of v1, /device:TPU:0, one launch (start us, length us, event | category | flops | bytes accessed | tf_op | source)
XLA Modules:
  0.0 1617.6 jit_solution(2815626947753380897)
XLA Ops:
  0.0 1601.9 %shard_map.28 = (bf16[640,13824]{1,0:T(8,128)(2,1)}, bf16[3,640,8192]{2,1,0:T(8,128)(2,1)}, bf16[4096,13824]{1,0:T(8,128)(2,1)}, f32[4,18,640,768]{3,2,1,0:T(8,1...) custom-call(bf16[640,32768]{1,0:T(8,128)(2,1)} %a_ref.1, ...), custom_call_target="tpu_custom_call" | custom-call | flops 579820584960 | bytes 1073741824 | tf_op jit(solution)/shard_map/pallas_call | solution.py:257
  1601.9 15.7 copy.4

commit v2 on v1

--- a/solution.py
+++ b/solution.py
@@ -18,7 +18,7 @@
 
 def _kernel(
     a_ref, b_ref, c_ref, a_got, b_got, part, first, fwd, last, summed,
-    a_v, b_v, acc, add_v, out_v,
+    a_v, b_v, acc, add_v, last_v,
     a_send, a_recv, b_send, b_recv, p_send, p_recv, load_sem, b_sem, acc_sem, add_sem,
 ):
     rows = a_ref.shape[0]
@@ -78,7 +78,7 @@
 
     own_loads = [
         pltpu.make_async_copy(
-            a_ref.at[:, a_cols(0, dc, 0)], a_v.at[2, :, pl.ds(dc * depth, depth)], load_sem.at[dc]
+            a_ref.at[:, a_cols(0, dc, 0)], a_v.at[0, :, pl.ds(dc * depth, depth)], load_sem.at[dc]
         )
         for dc in range(2)
     ]
@@ -95,7 +95,7 @@
     def hop(par, dst, src, t, kind):
         return pltpu.make_async_remote_copy(
             src_ref=src,
-            dst_ref=dst.at[t],
+            dst_ref=dst,
             send_sem=p_send.at[kind, t],
             recv_sem=p_recv.at[kind, t],
             device_id={"dp": ((x + 1 - par) % 2) * 2 + core, "tp": (y + par) % 2},
@@ -123,7 +123,7 @@
             acc_out(i).wait()
             if dst is not None:
                 par, t = place(i)
-                hop(par, dst, part.at[which, t], t, which - FIRST).start()
+                hop(par, dst.at[t], part.at[which, t], t, which - FIRST).start()
 
         for load in b_loads(0):
             load.start()
@@ -174,24 +174,32 @@
             copy.wait_recv()
         return pltpu.make_async_copy(a_got.at[g], a_v.at[slot], load_sem.at[slot])
 
-    phase(OWN, lambda par: 2, None)
+    phase(OWN, lambda par: 0, None)
     loads = [fetch(0, 0), fetch(1, 1)]
     for load in loads:
         load.start()
     for load in loads:
         load.wait()
     phase(FIRST, lambda par: par, first)
-    load = fetch(2, 2)
+    load = fetch(2, 0)
     load.start()
     load.wait()
-    phase(DIAG, lambda par: 2, fwd)
+    phase(DIAG, lambda par: 0, fwd)
+    load = pltpu.make_async_copy(a_got.at[0], a_v.at[0], load_sem.at[0])
+    load.start()
+    load.wait()
     phase(SECOND, lambda par: 1 - par, None)
+
+    def last_hop(i):
+        par, t = place(i)
+        dst = last.at[t] if not isinstance(i, int) or i < TILES - 2 else last_v.at[par]
+        return hop(1 - par, dst, summed.at[t], t, 2)
 
     def forward(i, carry):
         par, t = place(i)
         mine = pltpu.make_async_copy(part.at[SECOND, t], add_v.at[0], add_sem.at[0])
         mine.start()
-        hop(par, fwd, part.at[DIAG, t], t, DIAG - FIRST).wait_recv()
+        hop(par, fwd.at[t], part.at[DIAG, t], t, 1).wait_recv()
         theirs = pltpu.make_async_copy(fwd.at[t], add_v.at[1], add_sem.at[1])
         theirs.start()
         mine.wait()
@@ -200,33 +208,42 @@
         out = pltpu.make_async_copy(add_v.at[2], summed.at[t], add_sem.at[2])
         out.start()
         out.wait()
-        hop(1 - par, last, summed.at[t], t, 2).start()
+        last_hop(i).start()
         return carry
 
-    lax.fori_loop(0, TILES, forward, 0)
-
-    def final(i, carry):
+    lax.fori_loop(0, TILES - 2, forward, 0)
+    for i in range(TILES - 2, TILES):
+        forward(i, 0)
+
+    def start_near(i, slot):
         par, t = place(i)
-        own = pltpu.make_async_copy(part.at[OWN, t], add_v.at[0], add_sem.at[0])
+        own = pltpu.make_async_copy(part.at[OWN, t], add_v.at[slot], add_sem.at[slot])
         own.start()
-        hop(par, first, part.at[FIRST, t], t, 0).wait_recv()
-        near = pltpu.make_async_copy(first.at[t], add_v.at[1], add_sem.at[1])
+        hop(par, first.at[t], part.at[FIRST, t], t, 0).wait_recv()
+        near = pltpu.make_async_copy(first.at[t], add_v.at[slot + 1], add_sem.at[slot + 1])
         near.start()
         own.wait()
         near.wait()
-        hop(1 - par, last, summed.at[t], t, 2).wait_recv()
-        far = pltpu.make_async_copy(last.at[t], add_v.at[2], add_sem.at[2])
+
+    def columns(i):
+        return pl.ds(pl.multiple_of(place(i)[1] * tn, tn), tn)
+
+    def final(i, carry):
+        start_near(i, 0)
+        last_hop(i).wait_recv()
+        far = pltpu.make_async_copy(last.at[place(i)[1]], add_v.at[2], add_sem.at[2])
         far.start()
         far.wait()
-        out_v[...] = (add_v[0] + add_v[1] + add_v[2]).astype(out_v.dtype)
-        out = pltpu.make_async_copy(
-            out_v, c_ref.at[:, pl.ds(pl.multiple_of(t * tn, tn), tn)], add_sem.at[3]
-        )
-        out.start()
-        out.wait()
+        c_ref[:, columns(i)] = (add_v[0] + add_v[1] + add_v[2]).astype(c_ref.dtype)
         return carry
 
-    lax.fori_loop(0, TILES, final, 0)
+    lax.fori_loop(0, TILES - 2, final, 0)
+    for n, i in enumerate(range(TILES - 2, TILES)):
+        start_near(i, n)
+        add_v[n] = add_v[n] + add_v[n + 1]
+    for n, i in enumerate(range(TILES - 2, TILES)):
+        last_hop(i).wait_recv()
+        c_ref[:, columns(i)] = (add_v[n] + last_v[n]).astype(c_ref.dtype)
 
     for copy in b_copies:
         copy.wait_send()
@@ -236,12 +253,14 @@
 
     def drain(i, carry):
         par, t = place(i)
-        hop(par, first, part.at[FIRST, t], t, 0).wait_send()
-        hop(par, fwd, part.at[DIAG, t], t, 1).wait_send()
-        hop(1 - par, last, summed.at[t], t, 2).wait_send()
+        hop(par, first.at[t], part.at[FIRST, t], t, 0).wait_send()
+        hop(par, fwd.at[t], part.at[DIAG, t], t, 1).wait_send()
+        last_hop(i).wait_send()
         return carry
 
-    lax.fori_loop(0, TILES, drain, 0)
+    lax.fori_loop(0, TILES - 2, drain, 0)
+    for i in range(TILES - 2, TILES):
+        drain(i, 0)
 
 
 def solution(mesh):
@@ -257,7 +276,7 @@
         outs = pl.pallas_call(
             _kernel,
             out_shape=[
-                jax.ShapeDtypeStruct((rows, cols), bf16),
+                pltpu.VMEM((rows, cols), bf16),
                 jax.ShapeDtypeStruct((3, rows, 2 * depth), bf16),
                 jax.ShapeDtypeStruct((depth, cols), bf16),
                 jax.ShapeDtypeStruct((4, TILES, rows, tn), f32),
@@ -267,13 +286,13 @@
                 tiles,
             ],
             in_specs=[hbm] * 2,
-            out_specs=[hbm] * 8,
+            out_specs=[pl.BlockSpec(memory_space=pltpu.VMEM)] + [hbm] * 7,
             scratch_shapes=[
-                pltpu.VMEM((3, rows, 2 * depth), bf16),
+                pltpu.VMEM((2, rows, 2 * depth), bf16),
                 pltpu.VMEM((2, 2, depth // KSTEPS, tn), bf16),
                 pltpu.VMEM((2, rows, tn), f32),
                 pltpu.VMEM((3, rows, tn), f32),
-                pltpu.VMEM((rows, tn), bf16),
+                pltpu.VMEM((2, rows, tn), f32),
                 pltpu.SemaphoreType.DMA((3, 2)),
                 pltpu.SemaphoreType.DMA((3, 2)),
                 pltpu.SemaphoreType.DMA((BCHUNKS,)),
@@ -283,10 +302,10 @@
                 pltpu.SemaphoreType.DMA((3,)),
                 pltpu.SemaphoreType.DMA((2, 2)),
                 pltpu.SemaphoreType.DMA((2,)),
-                pltpu.SemaphoreType.DMA((4,)),
+                pltpu.SemaphoreType.DMA((3,)),
             ],
             compiler_params=pltpu.CompilerParams(
-                collective_id=0, has_side_effects=True, vmem_limit_bytes=60 * 2**20
+                collective_id=0, has_side_effects=True, vmem_limit_bytes=44 * 2**20
             ),
             cost_estimate=pl.CostEstimate(
                 flops=2 * rows * inner * cols, bytes_accessed=2**30, transcendentals=0

time: 1620 us -> 1600 us (0.988)
  no operation moved by 1% of the time
where the time goes in v2:
time: 1600 us
  Pallas kernels  1590 us (99%)
    pallas_call x1, Pallas kernels, local_block(): pl.pallas_call(_kernel, out_shape=[pltpu.VMEM((rows, cols), bf16), jax.Sh...  1590 us

profile of v2, /device:TPU:0, one launch (start us, length us, event | category | flops | bytes accessed | tf_op | source)
XLA Modules:
  0.0 1601.0 jit_solution(16025702669049961009)
XLA Ops:
  0.0 1594.5 %shard_map.28 = (bf16[640,13824]{1,0:T(8,128)(2,1)S(1)}, bf16[3,640,8192]{2,1,0:T(8,128)(2,1)}, bf16[4096,13824]{1,0:T(8,128)(2,1)}, f32[4,18,640,768]{3,2,1,0:T...) custom-call(bf16[640,32768]{1,0:T(8,128)(2,1)} %a_ref.1, ...), custom_call_target="tpu_custom_call" | custom-call | flops 579820584960 | bytes 1073741824 | tf_op jit(solution)/shard_map/pallas_call | solution.py:276
  1594.5 6.5 copy.4

commit v3 on v2

--- a/solution.py
+++ b/solution.py
@@ -13,13 +13,14 @@
 KSTEPS = 4
 BCHUNKS = 4
 WIDE = 256
+BANDS = 4
 OWN, FIRST, DIAG, SECOND = 0, 1, 2, 3
 
 
 def _kernel(
-    a_ref, b_ref, c_ref, a_got, b_got, part, first, fwd, last, summed,
-    a_v, b_v, acc, add_v, last_v,
-    a_send, a_recv, b_send, b_recv, p_send, p_recv, load_sem, b_sem, acc_sem, add_sem,
+    a_ref, b_ref, c_ref, near_v, last_v, a_got, b_got, part, first, fwd, last, summed,
+    a_v, b_v, acc,
+    a_send, a_recv, b_send, b_recv, p_send, p_recv, load_sem, b_sem, acc_sem, add_sem, across,
 ):
     rows = a_ref.shape[0]
     depth, cols = b_ref.shape
@@ -38,9 +39,10 @@
         return pl.ds(pl.multiple_of(block * depth, depth), depth)
 
     barrier = pltpu.get_barrier_semaphore()
-    for d in ((1, 0, 0), (0, 0, 1), (1, 0, 1), (0, 1, 0)):
+    for d in ((1, 0, 0), (0, 0, 1), (0, 1, 0)):
         pl.semaphore_signal(barrier, inc=1, device_id=device(*d), device_id_type=MESH)
-    pl.semaphore_wait(barrier, 4)
+    pl.semaphore_wait(barrier, 3)
+    pl.semaphore_signal(across, inc=1, device_id=device(1, 0, 0), device_id_type=MESH)
 
     bc = depth // BCHUNKS
     b_copies = [
@@ -73,6 +75,7 @@
     for dc in range(2):
         a_copies[0][dc].start()
         a_copies[1][dc].start()
+    pl.semaphore_wait(across, 1)
     for dc in range(2):
         a_copies[2][dc].start()
 
@@ -190,6 +193,8 @@
     load.wait()
     phase(SECOND, lambda par: 1 - par, None)
 
+    add_v = acc
+
     def last_hop(i):
         par, t = place(i)
         dst = last.at[t] if not isinstance(i, int) or i < TILES - 2 else last_v.at[par]
@@ -204,8 +209,8 @@
         theirs.start()
         mine.wait()
         theirs.wait()
-        add_v[2] = add_v[0] + add_v[1]
-        out = pltpu.make_async_copy(add_v.at[2], summed.at[t], add_sem.at[2])
+        add_v[0] = add_v[0] + add_v[1]
+        out = pltpu.make_async_copy(add_v.at[0], summed.at[t], add_sem.at[0])
         out.start()
         out.wait()
         last_hop(i).start()
@@ -215,36 +220,31 @@
     for i in range(TILES - 2, TILES):
         forward(i, 0)
 
-    def start_near(i, slot):
+    def near_terms(i):
         par, t = place(i)
-        own = pltpu.make_async_copy(part.at[OWN, t], add_v.at[slot], add_sem.at[slot])
+        own = pltpu.make_async_copy(part.at[OWN, t], add_v.at[0], add_sem.at[0])
         own.start()
         hop(par, first.at[t], part.at[FIRST, t], t, 0).wait_recv()
-        near = pltpu.make_async_copy(first.at[t], add_v.at[slot + 1], add_sem.at[slot + 1])
+        near = pltpu.make_async_copy(first.at[t], add_v.at[1], add_sem.at[1])
         near.start()
         own.wait()
         near.wait()
-
-    def columns(i):
-        return pl.ds(pl.multiple_of(place(i)[1] * tn, tn), tn)
+        return add_v[0] + add_v[1]
 
     def final(i, carry):
-        start_near(i, 0)
+        _, t = place(i)
+        add_v[0] = near_terms(i)
         last_hop(i).wait_recv()
-        far = pltpu.make_async_copy(last.at[place(i)[1]], add_v.at[2], add_sem.at[2])
+        far = pltpu.make_async_copy(last.at[t], add_v.at[1], add_sem.at[1])
         far.start()
         far.wait()
-        c_ref[:, columns(i)] = (add_v[0] + add_v[1] + add_v[2]).astype(c_ref.dtype)
+        at = pl.ds(pl.multiple_of(t * tn, tn), tn)
+        c_ref[:, at] = (add_v[0] + add_v[1]).astype(c_ref.dtype)
         return carry
 
     lax.fori_loop(0, TILES - 2, final, 0)
     for n, i in enumerate(range(TILES - 2, TILES)):
-        start_near(i, n)
-        add_v[n] = add_v[n] + add_v[n + 1]
-    for n, i in enumerate(range(TILES - 2, TILES)):
-        last_hop(i).wait_recv()
-        c_ref[:, columns(i)] = (add_v[n] + last_v[n]).astype(c_ref.dtype)
-
+        near_v[n] = near_terms(i)
     for copy in b_copies:
         copy.wait_send()
     for pair in a_copies:
@@ -261,6 +261,28 @@
     lax.fori_loop(0, TILES - 2, drain, 0)
     for i in range(TILES - 2, TILES):
         drain(i, 0)
+        last_hop(i).wait_recv()
+
+
+def _close(c_v, near_v, last_v, c_ref, out_v, sem, out_sem):
+    rows, cols = c_ref.shape
+    tn = cols // TILES
+    band = rows // BANDS
+    copies = []
+    for h in range(2):
+        at = pl.ds(h * HALF * tn, (HALF - 1) * tn)
+        for r in range(BANDS):
+            where = (pl.ds(r * band, band), at)
+            copies.append(pltpu.make_async_copy(c_v.at[where], c_ref.at[where], sem.at[h, r]))
+    for copy in copies:
+        copy.start()
+    for h in range(2):
+        out_v[h] = (near_v[h] + last_v[h]).astype(out_v.dtype)
+        at = pl.ds((h * HALF + HALF - 1) * tn, tn)
+        copies.append(pltpu.make_async_copy(out_v.at[h], c_ref.at[:, at], out_sem.at[h]))
+        copies[-1].start()
+    for copy in copies:
+        copy.wait()
 
 
 def solution(mesh):
@@ -271,12 +293,14 @@
         depth, cols = b_rows.shape
         tn = cols // TILES
         f32, bf16 = jnp.float32, a_rows.dtype
-        hbm = pl.BlockSpec(memory_space=pl.ANY)
+        hbm, vmem = pl.BlockSpec(memory_space=pl.ANY), pl.BlockSpec(memory_space=pltpu.VMEM)
         tiles = jax.ShapeDtypeStruct((TILES, rows, tn), f32)
         outs = pl.pallas_call(
             _kernel,
             out_shape=[
                 pltpu.VMEM((rows, cols), bf16),
+                pltpu.VMEM((2, rows, tn), f32),
+                pltpu.VMEM((2, rows, tn), f32),
                 jax.ShapeDtypeStruct((3, rows, 2 * depth), bf16),
                 jax.ShapeDtypeStruct((depth, cols), bf16),
                 jax.ShapeDtypeStruct((4, TILES, rows, tn), f32),
@@ -286,12 +310,10 @@
                 tiles,
             ],
             in_specs=[hbm] * 2,
-            out_specs=[pl.BlockSpec(memory_space=pltpu.VMEM)] + [hbm] * 7,
+            out_specs=[vmem] * 3 + [hbm] * 7,
             scratch_shapes=[
                 pltpu.VMEM((2, rows, 2 * depth), bf16),
                 pltpu.VMEM((2, 2, depth // KSTEPS, tn), bf16),
-                pltpu.VMEM((2, rows, tn), f32),
-                pltpu.VMEM((3, rows, tn), f32),
                 pltpu.VMEM((2, rows, tn), f32),
                 pltpu.SemaphoreType.DMA((3, 2)),
                 pltpu.SemaphoreType.DMA((3, 2)),
@@ -302,15 +324,28 @@
                 pltpu.SemaphoreType.DMA((3,)),
                 pltpu.SemaphoreType.DMA((2, 2)),
                 pltpu.SemaphoreType.DMA((2,)),
-                pltpu.SemaphoreType.DMA((3,)),
+                pltpu.SemaphoreType.DMA((2,)),
+                pltpu.SemaphoreType.REGULAR,
             ],
             compiler_params=pltpu.CompilerParams(
-                collective_id=0, has_side_effects=True, vmem_limit_bytes=44 * 2**20
+                collective_id=0, has_side_effects=True, vmem_limit_bytes=37 * 2**20
             ),
             cost_estimate=pl.CostEstimate(
                 flops=2 * rows * inner * cols, bytes_accessed=2**30, transcendentals=0
             ),
         )(a_rows, b_rows)
-        return outs[0]
+        held = [pltpu.with_memory_space_constraint(v, pltpu.VMEM) for v in outs[:3]]
+        return pl.pallas_call(
+            _close,
+            out_shape=jax.ShapeDtypeStruct((rows, cols), bf16),
+            in_specs=[vmem] * 3,
+            out_specs=hbm,
+            scratch_shapes=[
+                pltpu.VMEM((2, rows, tn), bf16),
+                pltpu.SemaphoreType.DMA((2, BANDS)),
+                pltpu.SemaphoreType.DMA((2,)),
+            ],
+            compiler_params=pltpu.CompilerParams(vmem_limit_bytes=8 * 2**20),
+        )(*held)
 
     return jax.shard_map(local_block, mesh=mesh, in_specs=(spec_rows, spec_rows), out_specs=spec_rows, check_vma=False)

time: 1600 us -> 1600 us (level)
    pallas_call x1 -> x2, Pallas kernels: 1590 us -> 1600 us  [the longest x1 1590 us: local_block(): pl.pallas_call(_kernel, out_shape=[pltpu.VMEM((rows, cols), bf16), pltpu....]
where the time goes in v3:
time: 1600 us
  Pallas kernels  1600 us (100%)
    pallas_call x1, Pallas kernels, local_block(): pl.pallas_call(_kernel, out_shape=[pltpu.VMEM((rows, cols), bf16), pltpu....  1590 us

profile of v3, /device:TPU:0, one launch (start us, length us, event | category | flops | bytes accessed | tf_op | source)
XLA Modules:
  0.0 1600.2 jit_solution(1096946414913842408)
XLA Ops:
  0.0 1593.9 %shard_map.28 = (bf16[640,13824]{1,0:T(8,128)(2,1)S(1)}, f32[2,640,768]{2,1,0:T(8,128)S(1)}, f32[2,640,768]{2,1,0:T(8,128)S(1)}, bf16[3,640,8192]{2,1,0:T(8,128)...) custom-call(bf16[640,32768]{1,0:T(8,128)(2,1)} %a_ref.1, ...), custom_call_target="tpu_custom_call" | custom-call | flops 579820584960 | bytes 1073741824 | tf_op jit(solution)/shard_map/pallas_call | solution.py:298
  1593.9 6.2 shard_map.29

commit v4 on v3

--- a/solution.py
+++ b/solution.py
@@ -13,14 +13,15 @@
 KSTEPS = 4
 BCHUNKS = 4
 WIDE = 256
-BANDS = 4
+BANDS = 8
+HEAD = 64
 OWN, FIRST, DIAG, SECOND = 0, 1, 2, 3
 
 
 def _kernel(
     a_ref, b_ref, c_ref, near_v, last_v, a_got, b_got, part, first, fwd, last, summed,
     a_v, b_v, acc,
-    a_send, a_recv, b_send, b_recv, p_send, p_recv, load_sem, b_sem, acc_sem, add_sem, across,
+    head_send, head_recv, head_sem, a_send, a_recv, b_send, b_recv, p_send, p_recv, load_sem, b_sem, acc_sem, add_sem, across,
 ):
     rows = a_ref.shape[0]
     depth, cols = b_ref.shape
@@ -37,6 +38,18 @@
     def a_cols(dx, dc, dy):
         block = ((x + dx) % 2) * 4 + ((core + dc) % 2) * 2 + (y + dy) % 2
         return pl.ds(pl.multiple_of(block * depth, depth), depth)
+
+    head = min(HEAD, rows // 2)
+    sides = ((1, 0), (0, 1), (1, 1))
+    staged = [a_v.at[1, pl.ds(g * head, head), pl.ds(0, depth)] for g in range(2)]
+    head_loads = [
+        pltpu.make_async_copy(
+            a_ref.at[pl.ds(0, head), a_cols(sides[g][0], 0, sides[g][1])], staged[g], head_sem.at[g]
+        )
+        for g in range(2)
+    ]
+    for load in head_loads:
+        load.start()
 
     barrier = pltpu.get_barrier_semaphore()
     for d in ((1, 0, 0), (0, 0, 1), (0, 1, 0)):
@@ -56,20 +69,35 @@
         )
         for j in range(BCHUNKS)
     ]
-    a_copies = [
-        [
-            pltpu.make_async_remote_copy(
-                src_ref=a_ref.at[:, a_cols(dx, dc, dy)],
-                dst_ref=a_got.at[g, :, pl.ds(dc * depth, depth)],
-                send_sem=a_send.at[g, dc],
-                recv_sem=a_recv.at[g, dc],
-                device_id=device(dx, 0, dy),
-                device_id_type=MESH,
-            )
-            for dc in range(2)
-        ]
-        for g, (dx, dy) in enumerate(((1, 0), (0, 1), (1, 1)))
+    heads = [
+        pltpu.make_async_remote_copy(
+            src_ref=staged[g],
+            dst_ref=a_got.at[g, pl.ds(0, head), pl.ds(0, depth)],
+            send_sem=head_send.at[g],
+            recv_sem=head_recv.at[g],
+            device_id=device(sides[g][0], 0, sides[g][1]),
+            device_id_type=MESH,
+        )
+        for g in range(2)
     ]
+
+    def a_copy(g, dc):
+        dx, dy = sides[g]
+        top = head if g < 2 and dc == 0 else 0
+        at = pl.ds(top, rows - top)
+        return pltpu.make_async_remote_copy(
+            src_ref=a_ref.at[at, a_cols(dx, dc, dy)],
+            dst_ref=a_got.at[g, at, pl.ds(dc * depth, depth)],
+            send_sem=a_send.at[g, dc],
+            recv_sem=a_recv.at[g, dc],
+            device_id=device(dx, 0, dy),
+            device_id_type=MESH,
+        )
+
+    a_copies = [[a_copy(g, dc) for dc in range(2)] for g in range(3)]
+    for load, copy in zip(head_loads, heads):
+        load.wait()
+        copy.start()
     for copy in b_copies:
         copy.start()
     for dc in range(2):
@@ -175,9 +203,13 @@
     def fetch(g, slot):
         for copy in a_copies[g]:
             copy.wait_recv()
+        if g < 2:
+            heads[g].wait_recv()
         return pltpu.make_async_copy(a_got.at[g], a_v.at[slot], load_sem.at[slot])
 
     phase(OWN, lambda par: 0, None)
+    for copy in heads:
+        copy.wait_send()
     loads = [fetch(0, 0), fetch(1, 1)]
     for load in loads:
         load.start()
@@ -315,6 +347,9 @@
                 pltpu.VMEM((2, rows, 2 * depth), bf16),
                 pltpu.VMEM((2, 2, depth // KSTEPS, tn), bf16),
                 pltpu.VMEM((2, rows, tn), f32),
+                pltpu.SemaphoreType.DMA((2,)),
+                pltpu.SemaphoreType.DMA((2,)),
+                pltpu.SemaphoreType.DMA((2,)),
                 pltpu.SemaphoreType.DMA((3, 2)),
                 pltpu.SemaphoreType.DMA((3, 2)),
                 pltpu.SemaphoreType.DMA((BCHUNKS,)),

time: 1600 us -> 1600 us (level)
  no operation moved by 1% of the time
where the time goes in v4:
time: 1600 us
  Pallas kernels  1600 us (100%)
    pallas_call x1, Pallas kernels, local_block(): pl.pallas_call(_kernel, out_shape=[pltpu.VMEM((rows, cols), bf16), pltpu....  1590 us

profile of v4, /device:TPU:0, one launch (start us, length us, event | category | flops | bytes accessed | tf_op | source)
XLA Modules:
  0.0 1600.6 jit_solution(9784250154554727430)
XLA Ops:
  0.0 1594.3 %shard_map.28 = (bf16[640,13824]{1,0:T(8,128)(2,1)S(1)}, f32[2,640,768]{2,1,0:T(8,128)S(1)}, f32[2,640,768]{2,1,0:T(8,128)S(1)}, bf16[3,640,8192]{2,1,0:T(8,128)...) custom-call(bf16[640,32768]{1,0:T(8,128)(2,1)} %a_ref.1, ...), custom_call_target="tpu_custom_call" | custom-call | flops 579820584960 | bytes 1073741824 | tf_op jit(solution)/shard_map/pallas_call | solution.py:330
  1594.3 6.3 shard_map.29

commit v5 on v3

--- a/solution.py
+++ b/solution.py
@@ -13,7 +13,7 @@
 KSTEPS = 4
 BCHUNKS = 4
 WIDE = 256
-BANDS = 4
+BANDS = 2
 OWN, FIRST, DIAG, SECOND = 0, 1, 2, 3
 
 
@@ -126,6 +126,12 @@
             acc_out(i).wait()
             if dst is not None:
                 par, t = place(i)
+                if which == FIRST:
+                    @pl.when(i == 1)
+                    def _():
+                        for copy in a_copies[2]:
+                            copy.wait_recv()
+
                 hop(par, dst.at[t], part.at[which, t], t, which - FIRST).start()
 
         for load in b_loads(0):
@@ -173,8 +179,9 @@
         finish(TILES - 1)
 
     def fetch(g, slot):
-        for copy in a_copies[g]:
-            copy.wait_recv()
+        if g < 2:
+            for copy in a_copies[g]:
+                copy.wait_recv()
         return pltpu.make_async_copy(a_got.at[g], a_v.at[slot], load_sem.at[slot])
 
     phase(OWN, lambda par: 0, None)

time: 1600 us -> 1600 us (level)
  no operation moved by 1% of the time
where the time goes in v5:
time: 1600 us
  Pallas kernels  1600 us (100%)
    pallas_call x1, Pallas kernels, local_block(): pl.pallas_call(_kernel, out_shape=[pltpu.VMEM((rows, cols), bf16), pltpu....  1590 us

profile of v5, /device:TPU:0, one launch (start us, length us, event | category | flops | bytes accessed | tf_op | source)
XLA Modules:
  0.0 1601.2 jit_solution(16846394783472480964)
XLA Ops:
  0.0 1594.9 %shard_map.28 = (bf16[640,13824]{1,0:T(8,128)(2,1)S(1)}, f32[2,640,768]{2,1,0:T(8,128)S(1)}, f32[2,640,768]{2,1,0:T(8,128)S(1)}, bf16[3,640,8192]{2,1,0:T(8,128)...) custom-call(bf16[640,32768]{1,0:T(8,128)(2,1)} %a_ref.1, ...), custom_call_target="tpu_custom_call" | custom-call | flops 579820584960 | bytes 1073741824 | tf_op jit(solution)/shard_map/pallas_call | solution.py:305
  1594.9 6.2 shard_map.29

commit v6 on v3

--- a/solution.py
+++ b/solution.py
@@ -13,7 +13,7 @@
 KSTEPS = 4
 BCHUNKS = 4
 WIDE = 256
-BANDS = 4
+BANDS = 8
 OWN, FIRST, DIAG, SECOND = 0, 1, 2, 3
 
 
@@ -264,23 +264,21 @@
         last_hop(i).wait_recv()
 
 
-def _close(c_v, near_v, last_v, c_ref, out_v, sem, out_sem):
+def _close(c_in, near_v, last_v, c_v, c_ref, sem):
+    del c_in
     rows, cols = c_ref.shape
     tn = cols // TILES
     band = rows // BANDS
     copies = []
-    for h in range(2):
-        at = pl.ds(h * HALF * tn, (HALF - 1) * tn)
-        for r in range(BANDS):
-            where = (pl.ds(r * band, band), at)
-            copies.append(pltpu.make_async_copy(c_v.at[where], c_ref.at[where], sem.at[h, r]))
-    for copy in copies:
-        copy.start()
-    for h in range(2):
-        out_v[h] = (near_v[h] + last_v[h]).astype(out_v.dtype)
-        at = pl.ds((h * HALF + HALF - 1) * tn, tn)
-        copies.append(pltpu.make_async_copy(out_v.at[h], c_ref.at[:, at], out_sem.at[h]))
-        copies[-1].start()
+    for r in range(BANDS):
+        at = pl.ds(r * band, band)
+        for h in range(2):
+            tile = pl.ds((h * HALF + HALF - 1) * tn, tn)
+            c_v[at, tile] = (near_v[h, at] + last_v[h, at]).astype(c_v.dtype)
+        if r:
+            copies[-1].start()
+        copies.append(pltpu.make_async_copy(c_v.at[at], c_ref.at[at], sem.at[r]))
+    copies[-1].start()
     for copy in copies:
         copy.wait()
 
@@ -337,15 +335,12 @@
         held = [pltpu.with_memory_space_constraint(v, pltpu.VMEM) for v in outs[:3]]
         return pl.pallas_call(
             _close,
-            out_shape=jax.ShapeDtypeStruct((rows, cols), bf16),
+            out_shape=[pltpu.VMEM((rows, cols), bf16), jax.ShapeDtypeStruct((rows, cols), bf16)],
             in_specs=[vmem] * 3,
-            out_specs=hbm,
-            scratch_shapes=[
-                pltpu.VMEM((2, rows, tn), bf16),
-                pltpu.SemaphoreType.DMA((2, BANDS)),
-                pltpu.SemaphoreType.DMA((2,)),
-            ],
+            out_specs=[vmem, hbm],
+            input_output_aliases={0: 0},
+            scratch_shapes=[pltpu.SemaphoreType.DMA((BANDS,))],
             compiler_params=pltpu.CompilerParams(vmem_limit_bytes=8 * 2**20),
-        )(*held)
+        )(*held)[1]
 
     return jax.shard_map(local_block, mesh=mesh, in_specs=(spec_rows, spec_rows), out_specs=spec_rows, check_vma=False)

time: 1600 us -> 1600 us (level)
  no operation moved by 1% of the time
where the time goes in v6:
time: 1600 us
  Pallas kernels  1600 us (100%)
    pallas_call x1, Pallas kernels, local_block(): pl.pallas_call(_kernel, out_shape=[pltpu.VMEM((rows, cols), bf16), pltpu....  1590 us

profile of v6, /device:TPU:0, one launch (start us, length us, event | category | flops | bytes accessed | tf_op | source)
XLA Modules:
  0.0 1600.2 jit_solution(6580816547176251501)
XLA Ops:
  0.0 1593.9 %shard_map.28 = (bf16[640,13824]{1,0:T(8,128)(2,1)S(1)}, f32[2,640,768]{2,1,0:T(8,128)S(1)}, f32[2,640,768]{2,1,0:T(8,128)S(1)}, bf16[3,640,8192]{2,1,0:T(8,128)...) custom-call(bf16[640,32768]{1,0:T(8,128)(2,1)} %a_ref.1, ...), custom_call_target="tpu_custom_call" | custom-call | flops 579820584960 | bytes 1073741824 | tf_op jit(solution)/shard_map/pallas_call | solution.py:296
  1593.9 6.3 shard_map.29

commit v7 on v3

--- a/solution.py
+++ b/solution.py
@@ -70,11 +70,12 @@
         ]
         for g, (dx, dy) in enumerate(((1, 0), (0, 1), (1, 1)))
     ]
+    for g in range(2):
+        a_copies[g][0].start()
     for copy in b_copies:
         copy.start()
-    for dc in range(2):
-        a_copies[0][dc].start()
-        a_copies[1][dc].start()
+    for g in range(2):
+        a_copies[g][1].start()
     pl.semaphore_wait(across, 1)
     for dc in range(2):
         a_copies[2][dc].start()

time: 1600 us -> 1600 us (level)
  no operation moved by 1% of the time
where the time goes in v7:
time: 1600 us
  Pallas kernels  1600 us (100%)
    pallas_call x1, Pallas kernels, local_block(): pl.pallas_call(_kernel, out_shape=[pltpu.VMEM((rows, cols), bf16), pltpu....  1590 us

profile of v7, /device:TPU:0, one launch (start us, length us, event | category | flops | bytes accessed | tf_op | source)
XLA Modules:
  0.0 1600.2 jit_solution(3095382950787392560)
XLA Ops:
  0.0 1593.9 %shard_map.28 = (bf16[640,13824]{1,0:T(8,128)(2,1)S(1)}, f32[2,640,768]{2,1,0:T(8,128)S(1)}, f32[2,640,768]{2,1,0:T(8,128)S(1)}, bf16[3,640,8192]{2,1,0:T(8,128)...) custom-call(bf16[640,32768]{1,0:T(8,128)(2,1)} %a_ref.1, ...), custom_call_target="tpu_custom_call" | custom-call | flops 579820584960 | bytes 1073741824 | tf_op jit(solution)/shard_map/pallas_call | solution.py:299
  1593.9 6.2 shard_map.29
